TPU v7x, 128 devices: a whole 4x4x4 slice. The times are simulated.
128 devices in a mesh: dp: 16 (over z, x), mp: 8 (over y, core).
Axes of the slice: x: 4, y: 4, z: 4, core: 2. Of those that a mesh axis runs over, the one named last changes fastest.
Arguments:
- tokens: bfloat16 [256, 4096], P('dp'), may hold values from -6 to 6
- norm_gain: float32 [4096], replicated, may hold values from 0.5 to 1.5
- router: bfloat16 [4096, 8], replicated, may hold values from -0.09375 to 0.09375
- w_gate: bfloat16 [8, 4096, 14336], P('mp', None, 'dp'), may hold values from -0.09375 to 0.09375
- w_up: bfloat16 [8, 4096, 14336], P('mp', None, 'dp'), may hold values from -0.09375 to 0.09375
- w_down: bfloat16 [8, 14336, 4096], P('mp', 'dp'), may hold values from -0.046875 to 0.046875
- final_gain: float32 [4096], replicated, may hold values from 0.5 to 1.5
- routes: int32 [256, 2], replicated, may hold values from 0 to 7, all different within a row; in each aligned block of 16 rows (0 to 15, 16 to 31, ...) at most 8 rows name the same one
- steer_hidden: bfloat16 [2, 256, 1024], P(None, 'dp'), may hold values from -6 to 6
- steer_query: bfloat16 [2, 256, 1024], P(None, 'dp', 'mp'), may hold values from -200 to 200
- steer_cache: bfloat16 [2, 2, 256, 64, 1024], P(None, None, 'dp', None, 'mp'), may hold values from -6 to 6
- steer_new: bfloat16 [2, 2, 256, 1024], P(None, None, 'dp', 'mp'), may hold values from -6 to 6
- cache_len: int32 [256], P('dp'), may hold values from 1 to 64
- steer_out: bfloat16 [2, 1024, 1024], P(None, 'mp'), may hold values from -0.1875 to 0.1875
- steer_gain: float32 [2, 1024], replicated, may hold values from 0.5 to 1.5
- base_head: bfloat16 [4096, 16000], P(None, ('dp', 'mp')), may hold values from -0.09375 to 0.09375
- steer_head: bfloat16 [2, 1024, 16000], P(None, None, ('dp', 'mp')), may hold values from -0.1875 to 0.1875
- inv_temp: float32 [256], replicated, may hold values from 0.5 to 40
Outputs:
- log_probs: float32 [256, 16000], P(None, ('dp', 'mp'))
Inputs may be any that keep to these rules, and one draw needn't show every extreme that they name: The two routes of a sequence differ; in every aligned block of 16 sequences (the sequences of one index of dp) no expert is named more than 8 times. Positions at and after cache_len[s] of sequence s's cache are unused.
All inputs are finite; a program needn't handle non-finite values.
Results may differ from a plain program's by a relative error of at most 0.00105.
Values may be sent and summed in bfloat16 or wider, within the bound.
A program may use at most 128 MiB of HBM per device.

v0:
```python
import math
import jax
import jax.numpy as jnp
from jax import lax
from jax.sharding import Mesh
from jax.sharding import PartitionSpec as P

HEAD_DIM = 128
MP = ("mp_0", "mp_1")
DP = ("dp_0", "dp_1")
DP_MP = ("dp_0", "dp_1", "mp_0", "mp_1")
steer_alpha = 2.0
norm_eps = 1e-05


def copy_for_each(x, axis):
    size = lax.axis_size(axis)
    return lax.all_to_all(jnp.broadcast_to(x[None], (size, *x.shape)), axis, 0, 0, tiled=True)


def over_copies(x, axis):
    everything = copy_for_each(x, axis)
    return jnp.sum(everything, axis=0)


def in_order(blocks, dim):
    blocks = jnp.moveaxis(blocks, 0, dim)
    dims = blocks.shape
    return blocks.reshape(*dims[:dim], dims[dim] * dims[dim + 1], *dims[dim + 2 :])


def gathered_copies(x, axis, dim):
    return in_order(copy_for_each(x, axis), dim)


def cut_along(x, dim, size):
    dims = x.shape
    blocks = x.reshape(*dims[:dim], size, dims[dim] // size, *dims[dim + 1 :])
    return jnp.moveaxis(blocks, dim, 0)


def sum_at_owner(x, axis, dim):
    size = lax.axis_size(axis)
    blocks = lax.all_to_all(cut_along(x, dim, size), axis, 0, 0, tiled=True)
    return jnp.sum(blocks.astype(jnp.float32), axis=0)


def taken_together(x, axis):
    everything = copy_for_each(x, axis)
    return jnp.sum(everything.astype(jnp.float32), axis=0)


def rows_first(arrays, axis, dims):
    turned = [jnp.moveaxis(a, dim, 0) for a, dim in zip(arrays, dims)]
    both = jnp.concatenate([t.reshape(len(t), -1) for t in turned], axis=1)
    filled, at, outs = (lax.all_gather(both, axis, axis=0, tiled=True), 0, [])
    for t, dim in zip(turned, dims):
        share = filled[:, at : at + t[0].size].reshape(-1, *t.shape[1:])
        outs.append(jnp.moveaxis(share, 0, dim))
        at += t[0].size
    return tuple(outs)


def collected_together(x, axis):
    leaves = jax.tree.leaves(x)
    turns = sorted(range(len(leaves)), key=lambda k: -leaves[k].size)
    width = (1, *leaves[turns[0]].shape)[-1]
    lines = [
        jnp.pad(leaves[k].reshape(-1), (0, -leaves[k].size % width)).reshape(-1, width)
        for k in turns
    ]
    both, at, found = (lax.all_gather(jnp.concatenate(lines), axis), 0, {})
    for k, line in zip(turns, lines):
        share = both[:, at : at + len(line)].reshape(len(both), -1)
        found[k] = share[:, : leaves[k].size].reshape(-1, *leaves[k].shape)
        at += len(line)
    numbers = iter(range(len(leaves)))
    return jax.tree.map(lambda _: found[next(numbers)], x)


def joined_all(x, axes, combine):
    for axis in axes:
        pieces = collected_together(x, axis)
        x = jax.tree.map(lambda part: part[0], pieces)
        for k in range(1, lax.axis_size(axis)):
            x = combine(x, jax.tree.map(lambda part: part[k], pieces))
    return x


def rms_scale(values, gain):
    mean_sq = jnp.mean(values * values, axis=-1, keepdims=True)
    return values * lax.rsqrt(mean_sq + norm_eps) * gain


def route_gates(normed, router, chosen, n_experts):
    logits = jnp.dot(normed, router, preferred_element_type=jnp.float32)
    marks = (chosen[:, :, None] == jnp.arange(n_experts, dtype=jnp.int32)[None, None, :]).astype(
        jnp.float32
    )
    picked = jnp.sum(logits[:, None, :] * marks, axis=2)
    first = 1.0 / (1.0 + jnp.exp(picked[:, 1] - picked[:, 0]))
    second = 1.0 / (1.0 + jnp.exp(picked[:, 0] - picked[:, 1]))
    return jnp.stack([first, second], axis=1)


def slot_tables(block_routes, block_gates, expert, capacity, n_experts):
    flat = block_routes.reshape(-1)
    marks = (flat[:, None] == jnp.arange(n_experts, dtype=jnp.int32)[None, :]).astype(jnp.int32)
    earlier = jnp.cumsum(marks, axis=0) - marks
    rank = jnp.sum(earlier * marks, axis=1).reshape(block_routes.shape)
    mine = block_routes == expert
    hits = (
        mine[:, :, None]
        & (rank[:, :, None] == jnp.arange(capacity, dtype=jnp.int32)[None, None, :])
    ).astype(jnp.float32)
    select = jnp.transpose(jnp.sum(hits, axis=1))
    combine = jnp.sum(hits * block_gates[:, :, None], axis=1)
    return (select, combine)


def swiglu(rows, gate_mat, up_mat):
    gate_part = jnp.dot(rows, gate_mat, preferred_element_type=jnp.float32)
    up_part = jnp.dot(rows, up_mat, preferred_element_type=jnp.float32)
    return (jax.nn.silu(gate_part) * up_part).astype(jnp.bfloat16)


def steer_attention(steer_query, steer_cache, steer_new, cache_len):
    models, seq_rows, width = steer_query.shape
    heads = width // HEAD_DIM
    span = steer_cache.shape[3]
    scale = 1.0 / math.sqrt(HEAD_DIM)
    queries = steer_query.reshape(models, seq_rows, heads, HEAD_DIM)
    keys = steer_cache[:, 0].reshape(models, seq_rows, span, heads, HEAD_DIM)
    values = steer_cache[:, 1].reshape(models, seq_rows, span, heads, HEAD_DIM)
    new_keys = steer_new[:, 0].reshape(models, seq_rows, heads, HEAD_DIM)
    new_values = steer_new[:, 1].reshape(models, seq_rows, heads, HEAD_DIM).astype(jnp.float32)
    scores = (
        jnp.einsum("mshd,msphd->mshp", queries, keys, preferred_element_type=jnp.float32) * scale
    )
    new_score = (
        jnp.einsum("mshd,mshd->msh", queries, new_keys, preferred_element_type=jnp.float32) * scale
    )
    live = (jnp.arange(span, dtype=jnp.int32)[None, :] < cache_len[:, None])[None, :, None, :]
    masked = jnp.where(live, scores, -1e30)
    summit = jnp.maximum(jnp.max(masked, axis=3), new_score)
    expo = jnp.where(live, jnp.exp(masked - summit[..., None]), 0.0)
    new_expo = jnp.exp(new_score - summit)
    denom = jnp.sum(expo, axis=3) + new_expo
    weights = (expo / denom[..., None]).astype(jnp.bfloat16)
    new_weight = (new_expo / denom).astype(jnp.bfloat16).astype(jnp.float32)
    attended = jnp.einsum("mshp,msphd->mshd", weights, values, preferred_element_type=jnp.float32)
    attended = attended + new_weight[..., None] * new_values
    return attended.reshape(models, seq_rows, width).astype(jnp.bfloat16)


def merge_pair(first, second):
    summit = jnp.maximum(first[0], second[0])
    return (summit, first[1] * jnp.exp(first[0] - summit) + second[1] * jnp.exp(second[0] - summit))


def per_device(
    tokens,
    norm_gain,
    router,
    w_gate,
    w_up,
    w_down,
    final_gain,
    routes,
    steer_hidden,
    steer_query,
    steer_cache,
    steer_new,
    cache_len,
    steer_out,
    steer_gain,
    base_head,
    steer_head,
    inv_temp,
):
    n_experts = lax.axis_size(MP)
    expert = lax.axis_index(MP)
    seq_rows = tokens.shape[0]
    capacity = 4 * seq_rows // n_experts
    gate_mat = w_gate[0]
    up_mat = w_up[0]
    down_mat = w_down[0]
    attended = steer_attention(steer_query, steer_cache, steer_new, cache_len)
    proj = jnp.einsum("msw,mwv->msv", attended, steer_out, preferred_element_type=jnp.float32)
    proj = over_copies(proj, MP)
    steer_state = steer_hidden.astype(jnp.float32) + proj
    steer_normed = rms_scale(steer_state, steer_gain[:, None, :]).astype(jnp.bfloat16)
    resid = tokens.astype(jnp.float32)
    normed = rms_scale(resid, norm_gain).astype(jnp.bfloat16)
    first_row = lax.axis_index(DP) * seq_rows
    own_routes = lax.dynamic_slice_in_dim(routes, first_row, seq_rows, 0)
    gates = route_gates(normed, router, own_routes, n_experts)
    select, combine = slot_tables(own_routes, gates, expert, capacity, n_experts)
    slot_in = jnp.dot(
        select.astype(jnp.bfloat16), normed, preferred_element_type=jnp.float32
    ).astype(jnp.bfloat16)
    hidden = swiglu(gathered_copies(slot_in, DP, 0), gate_mat, up_mat)
    slot_out = sum_at_owner(
        jnp.dot(hidden, down_mat, preferred_element_type=jnp.float32).astype(jnp.bfloat16), DP, 0
    )
    mixed = jnp.dot(combine, slot_out, precision=lax.Precision.HIGHEST)
    moe = taken_together(mixed.astype(jnp.bfloat16), MP).astype(jnp.float32)
    base_normed = rms_scale(resid + moe, final_gain).astype(jnp.bfloat16)
    base_all, steer_all = rows_first((base_normed[None], steer_normed), DP, (1, 1))
    base_all = base_all[0]
    base_logits = jnp.dot(base_all, base_head, preferred_element_type=jnp.float32)
    plus = jnp.dot(steer_all[0], steer_head[0], preferred_element_type=jnp.float32)
    minus = jnp.dot(steer_all[1], steer_head[1], preferred_element_type=jnp.float32)
    combined = inv_temp[:, None] * (base_logits + steer_alpha * (plus - minus))
    local_peak = jnp.max(combined, axis=1)
    local_total = jnp.sum(jnp.exp(combined - local_peak[:, None]), axis=1)
    peak_val, total = joined_all((local_peak, local_total), DP_MP, merge_pair)
    return combined - peak_val[:, None] - jnp.log(total)[:, None]


def solution(mesh):
    finer = Mesh(mesh.devices.reshape(4, 4, 4, 2), ("dp_0", "dp_1", "mp_0", "mp_1"))
    placed = (
        P(DP, None),
        P(),
        P(),
        P(MP, None, DP),
        P(MP, None, DP),
        P(MP, DP, None),
        P(),
        P(),
        P(None, DP, None),
        P(None, DP, MP),
        P(None, None, DP, None, MP),
        P(None, None, DP, MP),
        P(DP),
        P(None, MP, None),
        P(),
        P(None, DP_MP),
        P(None, None, DP_MP),
        P(),
    )
    return jax.shard_map(
        per_device, mesh=finer, in_specs=placed, out_specs=P(None, DP_MP), check_vma=False
    )
```

profile of v0, /device:TPU:1, one launch (start us, length us, event | category | flops | bytes accessed | tf_op | source)
XLA Modules:
  0.0 206.8 jit_solution(15885888711797221466)
XLA Ops:
  6.5 1.1 fusion.41
  8.5 1.1 fusion.49
  10.3 1.1 convolution_convert_fusion.1
  12.6 8.4 %all-to-all-start = ((bf16[16,8,4096]{2,1,0:T(8,128)(2,1)}), bf16[16,8,4096]{2,1,0:T(8,128)(2,1)S(1)}, u32[]{:S(2)}, u32[]{:S(2)}) async-start(bf16[16,8,4096]{2,1,0:T(8,128)(2,1)} %broadcast_in_dim.24), calls=%async_computation | async-start | bytes 2097152 | tf_op jit(solution)/shard_map/all_to_all | solution.py:18
  22.5 1.4 fusion.32
  24.0 13.0 %all-to-all-done = bf16[16,8,4096]{2,1,0:T(8,128)(2,1)S(1)} async-done(((bf16[16,8,4096]{2,1,0:T(8,128)(2,1)}), bf16[16,8,4096]{2,1,0:T(8,128)(2,1)S(1)}, u32[]{:S(2)}, u32[]{:S(2)}) %all-to-all-start) | async-done | bytes 1048608 | tf_op jit(solution)/shard_map/all_to_all | solution.py:18
  37.0 4.3 %fusion.4 = f32[128,896]{1,0:T(8,128)S(1)} fusion(bf16[1,4096,896]{2,1,0:T(8,128)(2,1)} %param.21, bf16[16,8,4096]{2,1,0:T(8,128)(2,1)S(1)} %all-to-all-done), kind=kOutput, calls=%fused_computation.4 | convolution fusion | flops 939524096 | bytes 8847360 | tf_op jit(solution)/shard_map/dot_general | solution.py:122
  41.4 8.6 %fusion.9 = bf16[16,8,4096]{2,1,0:T(8,128)(2,1)} fusion(bf16[1,896,4096]{2,1,0:T(8,128)(2,1)} %param.23, bf16[1,4096,896]{2,1,0:T(8,128)(2,1)} %param.22, bf16[16,8,4096]{2,1,0:T(8,128)(2,1)S(1)} %all-to-all-done, f32[128,896]{1,0:T(8,128)S(1)} %fusion.4), kind=kOutput, calls=%fused_computation.7 | convolution fusion | flops 1880260608 | bytes 17235968 | tf_op jit(solution)/shard_map/dot_general | solution.py:204
  50.1 4.3 %all-to-all-start.1 = ((bf16[16,8,4096]{2,1,0:T(8,128)(2,1)}), bf16[16,8,4096]{2,1,0:T(8,128)(2,1)S(1)}, u32[]{:S(2)}, u32[]{:S(2)}) async-start(bf16[16,8,4096]{2,1,0:T(8,128)(2,1)} %fusion.9), calls=%async_computation.1 | async-start | bytes 2097152 | tf_op jit(solution)/shard_map/all_to_all | solution.py:44
  54.7 1.3 fusion.30
  56.2 13.3 %all-to-all-done.1 = bf16[16,8,4096]{2,1,0:T(8,128)(2,1)S(1)} async-done(((bf16[16,8,4096]{2,1,0:T(8,128)(2,1)}), bf16[16,8,4096]{2,1,0:T(8,128)(2,1)S(1)}, u32[]{:S(2)}, u32[]{:S(2)}) %all-to-all-start.1) | async-done | bytes 1048608 | tf_op jit(solution)/shard_map/all_to_all | solution.py:44
  70.7 7.7 %all-to-all-start.3 = ((f32[8,2,16,1024]{3,2,1,0:T(8,128)}), f32[8,2,16,1024]{3,2,1,0:T(8,128)S(1)}, u32[]{:S(2)}, u32[]{:S(2)}) async-start(f32[8,2,16,1024]{3,2,1,0:T(8,128)} %broadcast_in_dim.29), calls=%async_computation.3 | async-start | bytes 2097152 | tf_op jit(solution)/shard_map/all_to_all | solution.py:18
  78.9 14.4 %all-to-all-done.3 = f32[8,2,16,1024]{3,2,1,0:T(8,128)S(1)} async-done(((f32[8,2,16,1024]{3,2,1,0:T(8,128)}), f32[8,2,16,1024]{3,2,1,0:T(8,128)S(1)}, u32[]{:S(2)}, u32[]{:S(2)}) %all-to-all-start.3) | async-done | bytes 1048608 | tf_op jit(solution)/shard_map/all_to_all | solution.py:18
  94.4 4.4 %all-to-all-start.2 = ((bf16[8,16,4096]{2,1,0:T(8,128)(2,1)}), bf16[8,16,4096]{2,1,0:T(8,128)(2,1)S(1)}, u32[]{:S(2)}, u32[]{:S(2)}) async-start(bf16[8,16,4096]{2,1,0:T(8,128)(2,1)} %broadcast_in_dim.25), calls=%async_computation.2 | async-start | bytes 2097152 | tf_op jit(solution)/shard_map/all_to_all | solution.py:18
  99.1 14.7 %all-to-all-done.2 = bf16[8,16,4096]{2,1,0:T(8,128)(2,1)S(1)} async-done(((bf16[8,16,4096]{2,1,0:T(8,128)(2,1)}), bf16[8,16,4096]{2,1,0:T(8,128)(2,1)S(1)}, u32[]{:S(2)}, u32[]{:S(2)}) %all-to-all-start.2) | async-done | bytes 1048608 | tf_op jit(solution)/shard_map/all_to_all | solution.py:18
  115.0 2.1 %fusion.109 = (bf16[1,1024,125]{1,0,2:T(2,128)(2,1)S(1)}, bf16[1,1024,125]{1,0,2:T(2,128)(2,1)S(1)}) fusion(bf16[2,1024,125]{1,0,2:T(2,128)(2,1)} %param.34), kind=kLoop, calls=%fused_computation.162 | loop fusion | bytes 1024000 | tf_op jit(solution)/shard_map/slice | solution.py:213
  118.6 39.7 %all-gather.10.cloned.1.call-done = bf16[256,6144]{1,0:T(8,128)(2,1)} async-done(((bf16[16,6144]{1,0:T(8,128)(2,1)}), bf16[256,6144]{1,0:T(8,128)(2,1)}) %all-gather.10.cloned.1.call-update) | async-done | bytes 3145744 | tf_op jit(solution)/shard_map/all_gather | solution.py:56
  158.4 1.3 slice.227
  160.2 1.2 fusion.29
  161.4 2.4 %fusion.12 = f32[256,125]{0,1:T(8,128)S(1)} fusion(bf16[4096,125]{1,0:T(8,128)(2,1)S(1)} %copy-done, bf16[256,6144]{1,0:T(8,128)(2,1)} %all-gather.10.cloned.1.call-done), kind=kOutput, calls=%fused_computation.10 | convolution fusion | flops 262144000 | bytes 3249152 | tf_op jit(solution)/shard_map/dot_general | solution.py:211
  164.2 8.1 %all-gather.4 = f32[4,2,256]{2,1,0:T(2,128)S(1)} all-gather(f32[1,2,256]{2,1,0:T(2,128)S(1)} %maximum_bitcast_fusion), channel_id=2, replica_groups=mesh['dp_0'=4,'dp_1'=4,'mp_0'=4,'mp_1'=2] {'dp_0'}, dimensions={0}, use_global_device_ids=true | all-gather | bytes 10240 | tf_op jit(solution)/shard_map/all_gather | solution.py:72
  172.4 8.1 %all-gather.5 = f32[4,2,256]{2,1,0:T(2,128)S(1)} all-gather(f32[1,2,256]{2,1,0:T(2,128)S(1)} %maximum_bitcast_fusion.1), channel_id=3, replica_groups=mesh['dp_0'=4,'dp_1'=4,'mp_0'=4,'mp_1'=2] {'dp_1'}, dimensions={0}, use_global_device_ids=true | all-gather | bytes 10240 | tf_op jit(solution)/shard_map/all_gather | solution.py:72
  180.6 8.5 %all-gather.6 = f32[4,2,256]{2,1,0:T(2,128)S(1)} all-gather(f32[1,2,256]{2,1,0:T(2,128)S(1)} %maximum_bitcast_fusion.2), channel_id=4, replica_groups=mesh['dp_0'=4,'dp_1'=4,'mp_0'=4,'mp_1'=2] {'mp_0'}, dimensions={0}, use_global_device_ids=true | all-gather | bytes 10240 | tf_op jit(solution)/shard_map/all_gather | solution.py:72
  189.1 10.1 %all-gather.7 = f32[2,2,256]{2,1,0:T(2,128)S(1)} all-gather(f32[1,2,256]{2,1,0:T(2,128)S(1)} %maximum_bitcast_fusion.3), channel_id=5, replica_groups=mesh['dp_0'=4,'dp_1'=4,'mp_0'=4,'mp_1'=2] {'mp_1'}, dimensions={0}, use_global_device_ids=true | all-gather | bytes 6144 | tf_op jit(solution)/shard_map/all_gather | solution.py:72
  (70 shorter events, 12.2 us)
Async XLA Ops:
  6.5 154.9 %copy-start = (bf16[4096,125]{1,0:T(8,128)(2,1)S(1)}, bf16[4096,125]{1,0:T(8,128)(2,1)}, u32[]{:S(2)}) copy-start(bf16[4096,125]{1,0:T(8,128)(2,1)} %param.33) | copy-start | bytes 3072004
  12.6 24.5 %all-to-all-start = ((bf16[16,8,4096]{2,1,0:T(8,128)(2,1)}), bf16[16,8,4096]{2,1,0:T(8,128)(2,1)S(1)}, u32[]{:S(2)}, u32[]{:S(2)}) async-start(bf16[16,8,4096]{2,1,0:T(8,128)(2,1)} %broadcast_in_dim.24), calls=%async_computation | async-start | bytes 2097152 | tf_op jit(solution)/shard_map/all_to_all | solution.py:18
  41.4 14.6 %copy-start.2 = (bf16[2,128,1024]{2,1,0:T(8,128)(2,1)S(1)}, bf16[2,128,1024]{2,1,0:T(8,128)(2,1)}, u32[]{:S(2)}) copy-start(bf16[2,128,1024]{2,1,0:T(8,128)(2,1)} %param.31) | copy-start | bytes 1572868
  41.4 14.6 %copy-start.4 = (bf16[2,2,16,128]{3,2,1,0:T(8,128)(2,1)S(1)}, bf16[2,2,16,128]{3,2,1,0:T(8,128)(2,1)}, u32[]{:S(2)}) copy-start(bf16[2,2,16,128]{3,2,1,0:T(8,128)(2,1)} %param.29) | copy-start | bytes 49156
  50.0 48.8 %copy-start.3 = (bf16[2,16,1024]{2,1,0:T(8,128)(2,1)S(1)}, bf16[2,16,1024]{2,1,0:T(8,128)(2,1)}, u32[]{:S(2)}) copy-start(bf16[2,16,1024]{2,1,0:T(8,128)(2,1)} %param.26) | copy-start | bytes 196612
  50.0 49.0 %copy-start.6 = (f32[2,1024]{1,0:T(2,128)S(1)}, f32[2,1024]{1,0:T(2,128)}, u32[]{:S(2)}) copy-start(f32[2,1024]{1,0:T(2,128)} %param.32) | copy-start | bytes 24580
  50.0 63.9 %copy-start.1 = (bf16[16,4096]{1,0:T(8,128)(2,1)S(1)}, bf16[16,4096]{1,0:T(8,128)(2,1)}, u32[]{:S(2)}) copy-start(bf16[16,4096]{1,0:T(8,128)(2,1)} %param.18) | copy-start | bytes 393220
  50.0 64.1 %copy-start.5 = (f32[4096]{0:T(1024)S(1)}, f32[4096]{0:T(1024)}, u32[]{:S(2)}) copy-start(f32[4096]{0:T(1024)} %param.24) | copy-start | bytes 49156
  50.1 19.5 %all-to-all-start.1 = ((bf16[16,8,4096]{2,1,0:T(8,128)(2,1)}), bf16[16,8,4096]{2,1,0:T(8,128)(2,1)S(1)}, u32[]{:S(2)}, u32[]{:S(2)}) async-start(bf16[16,8,4096]{2,1,0:T(8,128)(2,1)} %fusion.9), calls=%async_computation.1 | async-start | bytes 2097152 | tf_op jit(solution)/shard_map/all_to_all | solution.py:44
  70.7 22.6 %all-to-all-start.3 = ((f32[8,2,16,1024]{3,2,1,0:T(8,128)}), f32[8,2,16,1024]{3,2,1,0:T(8,128)S(1)}, u32[]{:S(2)}, u32[]{:S(2)}) async-start(f32[8,2,16,1024]{3,2,1,0:T(8,128)} %broadcast_in_dim.29), calls=%async_computation.3 | async-start | bytes 2097152 | tf_op jit(solution)/shard_map/all_to_all | solution.py:18
  94.4 19.4 %all-to-all-start.2 = ((bf16[8,16,4096]{2,1,0:T(8,128)(2,1)}), bf16[8,16,4096]{2,1,0:T(8,128)(2,1)S(1)}, u32[]{:S(2)}, u32[]{:S(2)}) async-start(bf16[8,16,4096]{2,1,0:T(8,128)(2,1)} %broadcast_in_dim.25), calls=%async_computation.2 | async-start | bytes 2097152 | tf_op jit(solution)/shard_map/all_to_all | solution.py:18
  98.8 59.5 %all-gather.10.cloned.1.call-start = ((), (), s32[]{:S(2)}) async-start(), calls=%async_computation.4 | async-start | bytes 3342336 | tf_op jit(solution)/shard_map/all_gather | solution.py:56
  99.1 64.7 %copy-start.7 = (f32[256]{0:T(256)S(1)}, f32[256]{0:T(256)}, u32[]{:S(2)}) copy-start(f32[256]{0:T(256)} %param.35) | copy-start | bytes 3076
Sparse Core Ops, SparseCore 0:
  115.1 43.2 all-gather.9
where the time goes:
time: 208 us; the launch traced here: 207 us
  waiting for transfers between devices  95.2 us (46%)
  blocking collectives  34.8 us (17%)
  starting transfers between devices  24.8 us (12%)
  matrix products  22.5 us (11%)
  between operations  13.7 us (7%)
  local copies, waits for them, and re-layouts  9.92 us (5%)
  other arithmetic  5.86 us (3%)
    all_to_all x3, waiting for transfers between devices, copy_for_each(): lax.all_to_all(jnp.broadcast_to(x[None], (size, *x.shape)), axis, 0, 0, t...  42.1 us
    all_gather x1, waiting for transfers between devices, rows_first(): filled, at, outs = (lax.all_gather(both, axis, axis=0, tiled=True), 0, [])  39.7 us
    all_gather x4, blocking collectives, collected_together(): both, at, found = (lax.all_gather(jnp.concatenate(lines), axis), 0, {})  34.8 us
    all_to_all x3, starting transfers between devices, copy_for_each(): lax.all_to_all(jnp.broadcast_to(x[None], (size, *x.shape)), axis, 0, 0, t...  20.5 us
    all_to_all x1, waiting for transfers between devices, sum_at_owner(): blocks = lax.all_to_all(cut_along(x, dim, size), axis, 0, 0, tiled=True)  13.3 us
    dot_general x1, matrix products, per_device(): jnp.dot(hidden, down_mat, preferred_element_type=jnp.float32)  8.64 us
    all_to_all x1, starting transfers between devices, sum_at_owner(): blocks = lax.all_to_all(cut_along(x, dim, size), axis, 0, 0, tiled=True)  4.35 us
    dot_general x1, matrix products, swiglu(): gate_part = jnp.dot(rows, gate_mat, preferred_element_type=jnp.float32)  4.34 us
  transfers between devices with their start and end apart: 5, of which 5 were waited for; matrix products, arithmetic and copies ran while one was open for 5% of the time, Pallas kernels for 0%

commit v1 on v0

--- a/solution.py
+++ b/solution.py
@@ -53,7 +53,13 @@
 def rows_first(arrays, axis, dims):
     turned = [jnp.moveaxis(a, dim, 0) for a, dim in zip(arrays, dims)]
     both = jnp.concatenate([t.reshape(len(t), -1) for t in turned], axis=1)
-    filled, at, outs = (lax.all_gather(both, axis, axis=0, tiled=True), 0, [])
+    filled, at, outs = (
+        jnp.concatenate(
+            lax.all_to_all(jnp.stack([both] * lax.axis_size(axis)), axis, 0, 0), axis=0
+        ),
+        0,
+        [],
+    )
     for t, dim in zip(turned, dims):
         share = filled[:, at : at + t[0].size].reshape(-1, *t.shape[1:])
         outs.append(jnp.moveaxis(share, 0, dim))

time: 208 us -> 203 us (0.976)
  between operations: 13.7 us -> 0.31 us
  waiting for transfers between devices: 95.2 us -> 99.9 us
  starting transfers between devices: 24.8 us -> 29.3 us
    all_to_all x0 -> x1, waiting for transfers between devices: none -> 44.5 us  [rows_first(): lax.all_to_all(jnp.stack([both] * lax.axis_size(axis)), axis, 0, 0)]
    all_gather x1 -> x0, waiting for transfers between devices: 39.7 us -> none  [rows_first(): filled, at, outs = (lax.all_gather(both, axis, axis=0, tiled=True), 0, [])]
    all_to_all x0 -> x1, starting transfers between devices: none -> 4.48 us  [rows_first(): lax.all_to_all(jnp.stack([both] * lax.axis_size(axis)), axis, 0, 0)]
  transfers between devices with their start and end apart: 5 -> 5, of which waited for: 5 -> 5; matrix products, arithmetic and copies ran while one was open for 5% -> 4% of each run, Pallas kernels for 0% -> 0%
where the time goes in v1:
time: 203 us; the launch traced here: 202 us
  waiting for transfers between devices  99.9 us (49%)
  blocking collectives  34.6 us (17%)
  starting transfers between devices  29.3 us (14%)
  matrix products  22.5 us (11%)
  local copies, waits for them, and re-layouts  10.6 us (5%)
  other arithmetic  5.16 us (3%)
    all_to_all x1, waiting for transfers between devices, rows_first(): lax.all_to_all(jnp.stack([both] * lax.axis_size(axis)), axis, 0, 0)  44.5 us
    all_to_all x3, waiting for transfers between devices, copy_for_each(): lax.all_to_all(jnp.broadcast_to(x[None], (size, *x.shape)), axis, 0, 0, t...  42.1 us
    all_gather x4, blocking collectives, collected_together(): both, at, found = (lax.all_gather(jnp.concatenate(lines), axis), 0, {})  34.6 us
    all_to_all x3, starting transfers between devices, copy_for_each(): lax.all_to_all(jnp.broadcast_to(x[None], (size, *x.shape)), axis, 0, 0, t...  20.5 us
    all_to_all x1, waiting for transfers between devices, sum_at_owner(): blocks = lax.all_to_all(cut_along(x, dim, size), axis, 0, 0, tiled=True)  13.3 us
    dot_general x1, matrix products, per_device(): jnp.dot(hidden, down_mat, preferred_element_type=jnp.float32)  8.64 us
    all_to_all x1, starting transfers between devices, rows_first(): lax.all_to_all(jnp.stack([both] * lax.axis_size(axis)), axis, 0, 0)  4.48 us
    all_to_all x1, starting transfers between devices, sum_at_owner(): blocks = lax.all_to_all(cut_along(x, dim, size), axis, 0, 0, tiled=True)  4.34 us
  transfers between devices with their start and end apart: 5, of which 5 were waited for; matrix products, arithmetic and copies ran while one was open for 4% of the time, Pallas kernels for 0%

profile of v1, /device:TPU:1, one launch (start us, length us, event | category | flops | bytes accessed | tf_op | source)
XLA Modules:
  0.0 202.4 jit_solution(16520374781583903837)
XLA Ops:
  0.0 1.1 fusion.41
  2.0 1.1 fusion.49
  6.0 8.4 %all-to-all-start = ((bf16[16,8,4096]{2,1,0:T(8,128)(2,1)}), bf16[16,8,4096]{2,1,0:T(8,128)(2,1)S(1)}, u32[]{:S(2)}, u32[]{:S(2)}) async-start(bf16[16,8,4096]{2,1,0:T(8,128)(2,1)} %broadcast_in_dim.24), calls=%async_computation | async-start | bytes 2097152 | tf_op jit(solution)/shard_map/all_to_all | solution.py:18
  16.0 1.4 fusion.32
  17.5 13.0 %all-to-all-done = bf16[16,8,4096]{2,1,0:T(8,128)(2,1)S(1)} async-done(((bf16[16,8,4096]{2,1,0:T(8,128)(2,1)}), bf16[16,8,4096]{2,1,0:T(8,128)(2,1)S(1)}, u32[]{:S(2)}, u32[]{:S(2)}) %all-to-all-start) | async-done | bytes 1048608 | tf_op jit(solution)/shard_map/all_to_all | solution.py:18
  30.5 4.3 %fusion.4 = f32[128,896]{1,0:T(8,128)S(1)} fusion(bf16[1,4096,896]{2,1,0:T(8,128)(2,1)} %param.21, bf16[16,8,4096]{2,1,0:T(8,128)(2,1)S(1)} %all-to-all-done), kind=kOutput, calls=%fused_computation.4 | convolution fusion | flops 939524096 | bytes 8847360 | tf_op jit(solution)/shard_map/dot_general | solution.py:128
  34.9 8.6 %fusion.9 = bf16[16,8,4096]{2,1,0:T(8,128)(2,1)} fusion(bf16[1,896,4096]{2,1,0:T(8,128)(2,1)} %param.23, bf16[1,4096,896]{2,1,0:T(8,128)(2,1)} %param.22, bf16[16,8,4096]{2,1,0:T(8,128)(2,1)S(1)} %all-to-all-done, f32[128,896]{1,0:T(8,128)S(1)} %fusion.4), kind=kOutput, calls=%fused_computation.7 | convolution fusion | flops 1880260608 | bytes 17235968 | tf_op jit(solution)/shard_map/dot_general | solution.py:210
  43.5 4.3 %all-to-all-start.1 = ((bf16[16,8,4096]{2,1,0:T(8,128)(2,1)}), bf16[16,8,4096]{2,1,0:T(8,128)(2,1)S(1)}, u32[]{:S(2)}, u32[]{:S(2)}) async-start(bf16[16,8,4096]{2,1,0:T(8,128)(2,1)} %fusion.9), calls=%async_computation.1 | async-start | bytes 2097152 | tf_op jit(solution)/shard_map/all_to_all | solution.py:44
  48.1 1.3 fusion.30
  49.7 13.3 %all-to-all-done.1 = bf16[16,8,4096]{2,1,0:T(8,128)(2,1)S(1)} async-done(((bf16[16,8,4096]{2,1,0:T(8,128)(2,1)}), bf16[16,8,4096]{2,1,0:T(8,128)(2,1)S(1)}, u32[]{:S(2)}, u32[]{:S(2)}) %all-to-all-start.1) | async-done | bytes 1048608 | tf_op jit(solution)/shard_map/all_to_all | solution.py:44
  64.1 7.7 %all-to-all-start.3 = ((f32[8,2,16,1024]{3,2,1,0:T(8,128)}), f32[8,2,16,1024]{3,2,1,0:T(8,128)S(1)}, u32[]{:S(2)}, u32[]{:S(2)}) async-start(f32[8,2,16,1024]{3,2,1,0:T(8,128)} %broadcast_in_dim.29), calls=%async_computation.3 | async-start | bytes 2097152 | tf_op jit(solution)/shard_map/all_to_all | solution.py:18
  72.4 14.4 %all-to-all-done.3 = f32[8,2,16,1024]{3,2,1,0:T(8,128)S(1)} async-done(((f32[8,2,16,1024]{3,2,1,0:T(8,128)}), f32[8,2,16,1024]{3,2,1,0:T(8,128)S(1)}, u32[]{:S(2)}, u32[]{:S(2)}) %all-to-all-start.3) | async-done | bytes 1048608 | tf_op jit(solution)/shard_map/all_to_all | solution.py:18
  87.9 4.4 %all-to-all-start.2 = ((bf16[8,16,4096]{2,1,0:T(8,128)(2,1)}), bf16[8,16,4096]{2,1,0:T(8,128)(2,1)S(1)}, u32[]{:S(2)}, u32[]{:S(2)}) async-start(bf16[8,16,4096]{2,1,0:T(8,128)(2,1)} %broadcast_in_dim.25), calls=%async_computation.2 | async-start | bytes 2097152 | tf_op jit(solution)/shard_map/all_to_all | solution.py:18
  92.6 14.7 %all-to-all-done.2 = bf16[8,16,4096]{2,1,0:T(8,128)(2,1)S(1)} async-done(((bf16[8,16,4096]{2,1,0:T(8,128)(2,1)}), bf16[8,16,4096]{2,1,0:T(8,128)(2,1)S(1)}, u32[]{:S(2)}, u32[]{:S(2)}) %all-to-all-start.2) | async-done | bytes 1048608 | tf_op jit(solution)/shard_map/all_to_all | solution.py:18
  107.7 2.1 %stack.5 = bf16[16,16,6144]{2,1,0:T(8,128)(2,1)} broadcast(bf16[16,6144]{1,0:T(8,128)(2,1)S(1)} %pad_maximum_fusion), dimensions={1,2} | broadcast | bytes 3342336 | tf_op jit(solution)/shard_map/stack | solution.py:58
  109.8 4.5 %all-to-all-start.4 = ((bf16[16,16,6144]{2,1,0:T(8,128)(2,1)}), bf16[16,16,6144]{2,1,0:T(8,128)(2,1)}, u32[]{:S(2)}, u32[]{:S(2)}) async-start(bf16[16,16,6144]{2,1,0:T(8,128)(2,1)} %stack.5), calls=%async_computation.4 | async-start | bytes 6291456 | tf_op jit(solution)/shard_map/all_to_all | solution.py:58
  116.6 44.5 %all-to-all-done.4 = bf16[16,16,6144]{2,1,0:T(8,128)(2,1)} async-done(((bf16[16,16,6144]{2,1,0:T(8,128)(2,1)}), bf16[16,16,6144]{2,1,0:T(8,128)(2,1)}, u32[]{:S(2)}, u32[]{:S(2)}) %all-to-all-start.4) | async-done | bytes 3145760 | tf_op jit(solution)/shard_map/all_to_all | solution.py:58
  161.1 1.3 slice.227
  162.9 2.4 %fusion.12 = f32[256,125]{0,1:T(8,128)S(1)} fusion(bf16[4096,125]{1,0:T(8,128)(2,1)S(1)} %copy-done, bf16[256,6144]{1,0:T(8,128)(2,1)} %bitcast.16), kind=kOutput, calls=%fused_computation.10 | convolution fusion | flops 262144000 | bytes 3249152 | tf_op jit(solution)/shard_map/dot_general | solution.py:217
  165.3 1.2 fusion.29
  166.9 8.1 %all-gather.4 = f32[4,2,256]{2,1,0:T(2,128)S(1)} all-gather(f32[1,2,256]{2,1,0:T(2,128)S(1)} %maximum_bitcast_fusion), channel_id=2, replica_groups=mesh['dp_0'=4,'dp_1'=4,'mp_0'=4,'mp_1'=2] {'dp_0'}, dimensions={0}, use_global_device_ids=true | all-gather | bytes 10240 | tf_op jit(solution)/shard_map/all_gather | solution.py:78
  175.1 8.1 %all-gather.5 = f32[4,2,256]{2,1,0:T(2,128)S(1)} all-gather(f32[1,2,256]{2,1,0:T(2,128)S(1)} %maximum_bitcast_fusion.1), channel_id=3, replica_groups=mesh['dp_0'=4,'dp_1'=4,'mp_0'=4,'mp_1'=2] {'dp_1'}, dimensions={0}, use_global_device_ids=true | all-gather | bytes 10240 | tf_op jit(solution)/shard_map/all_gather | solution.py:78
  183.3 8.1 %all-gather.6 = f32[4,2,256]{2,1,0:T(2,128)S(1)} all-gather(f32[1,2,256]{2,1,0:T(2,128)S(1)} %maximum_bitcast_fusion.2), channel_id=4, replica_groups=mesh['dp_0'=4,'dp_1'=4,'mp_0'=4,'mp_1'=2] {'mp_0'}, dimensions={0}, use_global_device_ids=true | all-gather | bytes 10240 | tf_op jit(solution)/shard_map/all_gather | solution.py:78
  191.5 10.2 %all-gather.7 = f32[2,2,256]{2,1,0:T(2,128)S(1)} all-gather(f32[1,2,256]{2,1,0:T(2,128)S(1)} %maximum_bitcast_fusion.3), channel_id=5, replica_groups=mesh['dp_0'=4,'dp_1'=4,'mp_0'=4,'mp_1'=2] {'mp_1'}, dimensions={0}, use_global_device_ids=true | all-gather | bytes 6144 | tf_op jit(solution)/shard_map/all_gather | solution.py:78
  (72 shorter events, 13.4 us)
Async XLA Ops:
  0.0 162.9 %copy-start = (bf16[4096,125]{1,0:T(8,128)(2,1)S(1)}, bf16[4096,125]{1,0:T(8,128)(2,1)}, u32[]{:S(2)}) copy-start(bf16[4096,125]{1,0:T(8,128)(2,1)} %param.33) | copy-start | bytes 3072004
  6.0 24.5 %all-to-all-start = ((bf16[16,8,4096]{2,1,0:T(8,128)(2,1)}), bf16[16,8,4096]{2,1,0:T(8,128)(2,1)S(1)}, u32[]{:S(2)}, u32[]{:S(2)}) async-start(bf16[16,8,4096]{2,1,0:T(8,128)(2,1)} %broadcast_in_dim.24), calls=%async_computation | async-start | bytes 2097152 | tf_op jit(solution)/shard_map/all_to_all | solution.py:18
  34.8 14.6 %copy-start.3 = (bf16[2,128,1024]{2,1,0:T(8,128)(2,1)S(1)}, bf16[2,128,1024]{2,1,0:T(8,128)(2,1)}, u32[]{:S(2)}) copy-start(bf16[2,128,1024]{2,1,0:T(8,128)(2,1)} %param.31) | copy-start | bytes 1572868
  34.9 14.6 %copy-start.5 = (bf16[2,2,16,128]{3,2,1,0:T(8,128)(2,1)S(1)}, bf16[2,2,16,128]{3,2,1,0:T(8,128)(2,1)}, u32[]{:S(2)}) copy-start(bf16[2,2,16,128]{3,2,1,0:T(8,128)(2,1)} %param.29) | copy-start | bytes 49156
  43.5 48.8 %copy-start.4 = (bf16[2,16,1024]{2,1,0:T(8,128)(2,1)S(1)}, bf16[2,16,1024]{2,1,0:T(8,128)(2,1)}, u32[]{:S(2)}) copy-start(bf16[2,16,1024]{2,1,0:T(8,128)(2,1)} %param.26) | copy-start | bytes 196612
  43.5 49.0 %copy-start.7 = (f32[2,1024]{1,0:T(2,128)S(1)}, f32[2,1024]{1,0:T(2,128)}, u32[]{:S(2)}) copy-start(f32[2,1024]{1,0:T(2,128)} %param.32) | copy-start | bytes 24580
  43.5 63.9 %copy-start.2 = (bf16[16,4096]{1,0:T(8,128)(2,1)S(1)}, bf16[16,4096]{1,0:T(8,128)(2,1)}, u32[]{:S(2)}) copy-start(bf16[16,4096]{1,0:T(8,128)(2,1)} %param.18) | copy-start | bytes 393220
  43.5 64.1 %copy-start.6 = (f32[4096]{0:T(1024)S(1)}, f32[4096]{0:T(1024)}, u32[]{:S(2)}) copy-start(f32[4096]{0:T(1024)} %param.24) | copy-start | bytes 49156
  43.5 19.5 %all-to-all-start.1 = ((bf16[16,8,4096]{2,1,0:T(8,128)(2,1)}), bf16[16,8,4096]{2,1,0:T(8,128)(2,1)S(1)}, u32[]{:S(2)}, u32[]{:S(2)}) async-start(bf16[16,8,4096]{2,1,0:T(8,128)(2,1)} %fusion.9), calls=%async_computation.1 | async-start | bytes 2097152 | tf_op jit(solution)/shard_map/all_to_all | solution.py:44
  64.1 22.6 %all-to-all-start.3 = ((f32[8,2,16,1024]{3,2,1,0:T(8,128)}), f32[8,2,16,1024]{3,2,1,0:T(8,128)S(1)}, u32[]{:S(2)}, u32[]{:S(2)}) async-start(f32[8,2,16,1024]{3,2,1,0:T(8,128)} %broadcast_in_dim.29), calls=%async_computation.3 | async-start | bytes 2097152 | tf_op jit(solution)/shard_map/all_to_all | solution.py:18
  87.9 19.4 %all-to-all-start.2 = ((bf16[8,16,4096]{2,1,0:T(8,128)(2,1)}), bf16[8,16,4096]{2,1,0:T(8,128)(2,1)S(1)}, u32[]{:S(2)}, u32[]{:S(2)}) async-start(bf16[8,16,4096]{2,1,0:T(8,128)(2,1)} %broadcast_in_dim.25), calls=%async_computation.2 | async-start | bytes 2097152 | tf_op jit(solution)/shard_map/all_to_all | solution.py:18
  92.4 21.9 %copy-start.1 = (bf16[2,1024,125]{1,0,2:T(2,128)(2,1)S(1)}, bf16[2,1024,125]{1,0,2:T(2,128)(2,1)}, u32[]{:S(2)}) copy-start(bf16[2,1024,125]{1,0,2:T(2,128)(2,1)} %param.34) | copy-start | bytes 1536004
  109.8 51.3 %all-to-all-start.4 = ((bf16[16,16,6144]{2,1,0:T(8,128)(2,1)}), bf16[16,16,6144]{2,1,0:T(8,128)(2,1)}, u32[]{:S(2)}, u32[]{:S(2)}) async-start(bf16[16,16,6144]{2,1,0:T(8,128)(2,1)} %stack.5), calls=%async_computation.4 | async-start | bytes 6291456 | tf_op jit(solution)/shard_map/all_to_all | solution.py:58
  114.3 52.3 %copy-start.8 = (f32[256]{0:T(256)S(1)}, f32[256]{0:T(256)}, u32[]{:S(2)}) copy-start(f32[256]{0:T(256)} %param.35) | copy-start | bytes 3076
